TPU v7x, 32 devices: a whole 2x2x4 slice. The times are simulated.
32 devices in a mesh: group: 4 (over z), batch: 8 (over y, x, core).
Axes of the slice: x: 2, y: 2, z: 4, core: 2. Of those that a mesh axis runs over, the one named last changes fastest.
Arguments:
- embeds: bfloat16 [65536, 256], P(('group', 'batch')), may hold values from -6 to 6
- out_grad: bfloat16 [65536, 256], P(('group', 'batch')), may hold values from -48 to 48
- w_query: bfloat16 [256, 256], replicated, may hold values from -0.375 to 0.375
- w_key: bfloat16 [256, 256], replicated, may hold values from -0.375 to 0.375
- w_value: bfloat16 [256, 256], replicated, may hold values from -0.375 to 0.375
- lengths: int32 [128], P(('group', 'batch')), may hold values from 1 to 512, as said below
- item_rows: int32 [65536], P(('group', 'batch')), may hold values from 0 to 2047, as said below
- tile_owner: int32 [512], P(('group', 'batch')), may hold values from 0 to 3, as said below
Outputs:
- table_grad: float32 [8192, 256], P(('group', 'batch'))
Inputs may be any that keep to these rules, and one draw needn't show every extreme that they name: `lengths`: a history's live tokens are its first positions; in every draw some history has exactly 512 live tokens. `tile_owner`: among the first 8 tiles of each device's own tiles, and among the last 8, every group owns exactly 2 tiles. `item_rows`: of the 128 tokens of each tile, at most 32 have rows r with the same r // 256, and in every tile some value of r // 256 is taken by exactly 32 tokens.
All inputs are finite; a program needn't handle non-finite values.
Results may differ from a plain program's by a relative error of at most 0.0024.
The roundings to bfloat16 on the way count: a program that leaves them out, or rounds other values in their place, can miss the bound.
Values may be sent and summed in bfloat16 or wider, within the bound.
No kernel may reach another device: no remote copies, remote signals or barrier semaphores. Data moves between devices by JAX's collectives and lax.ppermute only.
A program may use at most 64 MiB of HBM per device.

v0:
```python
import math
import jax
import jax.numpy as jnp
from jax import lax
from jax.sharding import PartitionSpec as P

HEADS = 2
TILE = 128
SEQ_LEN = 512
ROWS_DEV = 256


def sequence_grads(query, key_rows, value, grad_out, count, w_query, w_key, w_value):
    span = query.shape[0]
    position = lax.broadcasted_iota(jnp.int32, (span, span), 0)
    other = lax.broadcasted_iota(jnp.int32, (span, span), 1)
    live = ((other <= position) & (position < count)).astype(jnp.float32)
    weight = live / count.astype(jnp.float32)
    scale = 1.0 / math.sqrt(query.shape[2])
    scores = jnp.einsum("ihd,jhd->hij", query, key_rows, preferred_element_type=jnp.float32) * scale
    sigma = jax.nn.sigmoid(scores)
    attend = (scores * sigma * weight).astype(jnp.bfloat16)
    value_grad = jnp.einsum(
        "hij,ihd->jhd", attend, grad_out, preferred_element_type=jnp.float32
    ).astype(jnp.bfloat16)
    attend_grad = jnp.einsum("ihd,jhd->hij", grad_out, value, preferred_element_type=jnp.float32)
    score_grad = (attend_grad * weight * sigma * (1.0 + scores * (1.0 - sigma))).astype(
        jnp.bfloat16
    )
    query_grad = (
        jnp.einsum("hij,jhd->ihd", score_grad, key_rows, preferred_element_type=jnp.float32) * scale
    ).astype(jnp.bfloat16)
    key_grad = (
        jnp.einsum("hij,ihd->jhd", score_grad, query, preferred_element_type=jnp.float32) * scale
    ).astype(jnp.bfloat16)
    width = w_query.shape[0]
    token = jnp.dot(query_grad.reshape(span, width), w_query.T, preferred_element_type=jnp.float32)
    token = token + jnp.dot(
        key_grad.reshape(span, width), w_key.T, preferred_element_type=jnp.float32
    )
    token = token + jnp.dot(
        value_grad.reshape(span, width), w_value.T, preferred_element_type=jnp.float32
    )
    return token.astype(jnp.bfloat16)


def token_grads(embeds, out_grad, w_query, w_key, w_value, lengths):
    history_count = lengths.shape[0]
    width = embeds.shape[1]
    head_size = width // HEADS

    def project(weight_matrix):
        return (
            jnp.dot(embeds, weight_matrix, preferred_element_type=jnp.float32)
            .astype(jnp.bfloat16)
            .reshape(history_count, SEQ_LEN, HEADS, head_size)
        )

    query = project(w_query)
    key_rows = project(w_key)
    value = project(w_value)
    grad_heads = out_grad.reshape(history_count, SEQ_LEN, HEADS, head_size)
    half_span = SEQ_LEN // 2

    def short_history(item):
        front = sequence_grads(
            item[0][:half_span],
            item[1][:half_span],
            item[2][:half_span],
            item[3][:half_span],
            item[4],
            w_query,
            w_key,
            w_value,
        )
        return jnp.concatenate(
            [front, jnp.zeros((SEQ_LEN - half_span, width), jnp.bfloat16)], axis=0
        )

    def whole_history(item):
        return sequence_grads(item[0], item[1], item[2], item[3], item[4], w_query, w_key, w_value)

    def one_history(item):
        return lax.cond(item[4] <= half_span, short_history, whole_history, item)

    result = lax.map(one_history, (query, key_rows, value, grad_heads, lengths))
    return result.reshape(history_count * SEQ_LEN, width)


def onehot_sum(row_count, tile_values, tile_rows, block_rows, initial):
    width = tile_values.shape[-1]
    flat_values = tile_values.reshape(-1, width)
    flat_rows = tile_rows.reshape(-1)
    step_count = flat_rows.shape[0] // block_rows
    target = lax.broadcasted_iota(jnp.int32, (row_count, 1), 0)

    def add_block(accum, item):
        onehot = (target == item[1][None, :]).astype(jnp.bfloat16)
        return (accum + jnp.dot(onehot, item[0], preferred_element_type=jnp.float32), None)

    blocks = (
        flat_values.reshape(step_count, block_rows, width),
        flat_rows.reshape(step_count, block_rows),
    )
    accum, unused = lax.scan(add_block, initial, blocks)
    return accum


def on_device(embeds, out_grad, w_query, w_key, w_value, lengths, item_rows, tile_owner):
    live_total = lax.psum(jnp.sum(lengths.astype(jnp.float32)), ("group", "batch"))
    device_count = lax.axis_size("group") * lax.axis_size("batch")
    scale_factor = embeds.shape[0] * device_count / live_total
    token_grad = token_grads(embeds, out_grad, w_query, w_key, w_value, lengths)
    width = token_grad.shape[1]
    ranking = jnp.argsort(tile_owner, stable=True)
    tile_values = token_grad.reshape(-1, TILE, width)[ranking]
    tile_rows = item_rows.reshape(-1, TILE)[ranking]
    got_values, got_rows = (
        lax.all_to_all(tile_values, "group", split_axis=0, concat_axis=0, tiled=True),
        lax.all_to_all(tile_rows, "group", split_axis=0, concat_axis=0, tiled=True),
    )
    empty_rows = jnp.zeros((ROWS_DEV * lax.axis_size("batch"), width), jnp.float32)
    table = lax.psum_scatter(
        onehot_sum(ROWS_DEV * lax.axis_size("batch"), got_values, got_rows, 4 * TILE, empty_rows),
        "batch",
        scatter_dimension=0,
        tiled=True,
    )
    return scale_factor * table


def solution(mesh):
    in_specs = (
        P(("group", "batch"), None),
        P(("group", "batch"), None),
        P(),
        P(),
        P(),
        P(("group", "batch")),
        P(("group", "batch")),
        P(("group", "batch")),
    )
    out_specs = P(("group", "batch"), None)
    return jax.shard_map(
        on_device, mesh=mesh, in_specs=in_specs, out_specs=out_specs, check_vma=False
    )
```

profile of v0, /device:TPU:0, one launch (start us, length us, event | category | flops | bytes accessed | tf_op | source)
XLA Modules:
  0.0 158.3 jit_solution(10579940593462021619)
XLA Ops:
  6.5 2.0 %sort.17 = (s32[16]{0:T(128)}, s32[16]{0:T(128)S(1)}) sort(s32[16]{0:T(128)} %param.21, s32[16]{0:T(128)S(1)} %iota.48), dimensions={0}, to_apply=%region_6.7 | sort | flops 64 | bytes 256 | tf_op jit(solution)/shard_map/jit(argsort)/sort | solution.py:115
  8.5 1.8 %gather_fusion = s32[16,128]{1,0:T(8,128)} fusion(s32[16,128]{1,0:T(8,128)} %bitcast.105, s32[1024]{0:T(1024)S(1)} %pad_clamp_fusion), kind=kCustom, calls=%fused_computation | custom fusion | bytes 16448 | tf_op jit(solution)/shard_map/gather | solution.py:117
  10.4 6.3 %all-to-all-start = ((s32[4,4,128]{2,1,0:T(4,128)}), s32[4,4,128]{2,1,0:T(4,128)S(1)}, u32[]{:S(2)}, u32[]{:S(2)}) async-start(s32[4,4,128]{2,1,0:T(4,128)} %bitcast.20), calls=%async_computation | async-start | bytes 16384 | tf_op jit(solution)/shard_map/all_to_all | solution.py:120
  16.7 2.2 %reshape.79 = bf16[4,512,2,128]{3,2,1,0:T(2,128)(2,1)} reshape(bf16[2048,256]{1,0:T(8,128)(2,1)} %param.15) | data formatting | bytes 2097152 | tf_op jit(solution)/shard_map/reshape | solution.py:62
  23.0 34.3 %while.21 = (s32[]{:T(128)}, bf16[4,512,256]{2,1,0:T(8,128)(2,1)}, s32[4]{0:T(128)S(1)}, bf16[4,512,2,128]{3,2,1,0:T(2,128)(2,1)S(1)}, bf16[4,512,2,128]{3,2,1,0...) while((s32[]{:T(128)}, bf16[4,512,256]{2,1,0:T(8,128)(2,1)}, ...), condition=%wide.region_5.6_spmd, body=%wide.region_2.5_spmd.sunk | while | flops 883687936 | bytes 23463240 | solution.py:86
  24.3 1.4 constant_dynamic-slice_fusion.8
  27.2 3.6 %conditional.2 = (bf16[1,512,256]{2,1,0:T(8,128)(2,1)S(1)}) conditional(s32[]{:T(128)} %convert_element_type.105, (bf16[512,2,128]{2,0,1:T(8,128)(2,1)S(1)}, bf16[512,2,128]{2,0,1:T(8,128)(2,1)S(1)}, s32[]{:T(128)}, bf16[512,2,128]{2,0,1:T(8,128)(2,1)S(1)}, bf16[512,2,128]{2,0,1:T(8,128)(2,1)S(1)}, /*index=5*/bf16[256,256]{1,0:T(8,128)(2,1)S(1)}, ...), branch_computations={%region_3.3_spmd, %region_4.4_spmd} | conditional | flops 883687936 | bytes 18744356 | solution.py:84
  32.9 1.4 constant_dynamic-slice_fusion.8
  35.8 3.6 %conditional.2 = (bf16[1,512,256]{2,1,0:T(8,128)(2,1)S(1)}) conditional(s32[]{:T(128)} %convert_element_type.105, (bf16[512,2,128]{2,0,1:T(8,128)(2,1)S(1)}, bf16[512,2,128]{2,0,1:T(8,128)(2,1)S(1)}, s32[]{:T(128)}, bf16[512,2,128]{2,0,1:T(8,128)(2,1)S(1)}, bf16[512,2,128]{2,0,1:T(8,128)(2,1)S(1)}, /*index=5*/bf16[256,256]{1,0:T(8,128)(2,1)S(1)}, ...), branch_computations={%region_3.3_spmd, %region_4.4_spmd} | conditional | flops 883687936 | bytes 18744356 | solution.py:84
  41.5 1.4 constant_dynamic-slice_fusion.8
  44.4 3.6 %conditional.2 = (bf16[1,512,256]{2,1,0:T(8,128)(2,1)S(1)}) conditional(s32[]{:T(128)} %convert_element_type.105, (bf16[512,2,128]{2,0,1:T(8,128)(2,1)S(1)}, bf16[512,2,128]{2,0,1:T(8,128)(2,1)S(1)}, s32[]{:T(128)}, bf16[512,2,128]{2,0,1:T(8,128)(2,1)S(1)}, bf16[512,2,128]{2,0,1:T(8,128)(2,1)S(1)}, /*index=5*/bf16[256,256]{1,0:T(8,128)(2,1)S(1)}, ...), branch_computations={%region_3.3_spmd, %region_4.4_spmd} | conditional | flops 883687936 | bytes 18744356 | solution.py:84
  50.1 1.4 constant_dynamic-slice_fusion.8
  53.0 3.6 %conditional.2 = (bf16[1,512,256]{2,1,0:T(8,128)(2,1)S(1)}) conditional(s32[]{:T(128)} %convert_element_type.105, (bf16[512,2,128]{2,0,1:T(8,128)(2,1)S(1)}, bf16[512,2,128]{2,0,1:T(8,128)(2,1)S(1)}, s32[]{:T(128)}, bf16[512,2,128]{2,0,1:T(8,128)(2,1)S(1)}, bf16[512,2,128]{2,0,1:T(8,128)(2,1)S(1)}, /*index=5*/bf16[256,256]{1,0:T(8,128)(2,1)S(1)}, ...), branch_computations={%region_3.3_spmd, %region_4.4_spmd} | conditional | flops 883687936 | bytes 18744356 | solution.py:84
  57.3 2.9 %gather_fusion.1 = bf16[16,128,256]{2,1,0:T(8,128)(2,1)} fusion(bf16[16,128,256]{2,1,0:T(8,128)(2,1)} %bitcast.104, s32[1024]{0:T(1024)S(1)} %pad_clamp_fusion), kind=kCustom, calls=%fused_computation.1 | custom fusion | bytes 2097216 | tf_op jit(solution)/shard_map/gather | solution.py:116
  60.2 5.1 %all-to-all-start.1 = ((bf16[16,128,256]{2,1,0:T(8,128)(2,1)}), bf16[16,128,256]{2,1,0:T(8,128)(2,1)}, u32[]{:S(2)}, u32[]{:S(2)}) async-start(bf16[16,128,256]{2,1,0:T(8,128)(2,1)} %gather_fusion.1), calls=%async_computation.1 | async-start | bytes 2097152 | tf_op jit(solution)/shard_map/all_to_all | solution.py:119
  65.3 25.3 %all-to-all-done.1 = bf16[16,128,256]{2,1,0:T(8,128)(2,1)} async-done(((bf16[16,128,256]{2,1,0:T(8,128)(2,1)}), bf16[16,128,256]{2,1,0:T(8,128)(2,1)}, u32[]{:S(2)}, u32[]{:S(2)}) %all-to-all-start.1) | async-done | bytes 1048608 | tf_op jit(solution)/shard_map/all_to_all | solution.py:119
  90.5 9.5 %while.22 = (s32[]{:T(128)}, f32[2048,256]{1,0:T(8,128)S(1)}, s32[4,512]{1,0:T(4,128)S(1)}, bf16[4,512,256]{2,1,0:T(8,128)(2,1)}, s32[]{:T(128)}, /*index=5*/s32[]{:T(128)}) while((s32[]{:T(128)}, f32[2048,256]{1,0:T(8,128)S(1)}, s32[4,512]{1,0:T(4,128)S(1)}, bf16[4,512,256]{2,1,0:T(8,128)(2,1)}, s32[]{:T(128)}, ...), condition=%wide.region_8.9_spmd.clone, body=%wide.region_7.8_spmd.clone.sunk | while | flops 538968064 | bytes 4462687 | solution.py:105
  90.5 2.3 %fusion.67 = f32[2048,256]{1,0:T(8,128)S(1)} fusion(f32[2048,256]{1,0:T(8,128)S(1)} %get-tuple-element.362, s32[512]{0:T(512)S(1)} %bitcast.106, pred[]{:T(512)S(6)} %compare.8, bf16[4,512,256]{2,1,0:T(8,128)(2,1)} %get-tuple-element.370, s32[]{:T(128)S(6)} %copy.74), kind=kOutput, calls=%fused_computation.60.clone.1 | convolution fusion | flops 538968064 | bytes 4458501 | tf_op jit(solution)/shard_map/while/body/eval_jaxpr/dot_general | solution.py:99
  92.9 2.3 %fusion.67 = f32[2048,256]{1,0:T(8,128)S(1)} fusion(f32[2048,256]{1,0:T(8,128)S(1)} %get-tuple-element.362, s32[512]{0:T(512)S(1)} %bitcast.106, pred[]{:T(512)S(6)} %compare.8, bf16[4,512,256]{2,1,0:T(8,128)(2,1)} %get-tuple-element.370, s32[]{:T(128)S(6)} %copy.74), kind=kOutput, calls=%fused_computation.60.clone.1 | convolution fusion | flops 538968064 | bytes 4458501 | tf_op jit(solution)/shard_map/while/body/eval_jaxpr/dot_general | solution.py:99
  95.3 2.3 %fusion.67 = f32[2048,256]{1,0:T(8,128)S(1)} fusion(f32[2048,256]{1,0:T(8,128)S(1)} %get-tuple-element.362, s32[512]{0:T(512)S(1)} %bitcast.106, pred[]{:T(512)S(6)} %compare.8, bf16[4,512,256]{2,1,0:T(8,128)(2,1)} %get-tuple-element.370, s32[]{:T(128)S(6)} %copy.74), kind=kOutput, calls=%fused_computation.60.clone.1 | convolution fusion | flops 538968064 | bytes 4458501 | tf_op jit(solution)/shard_map/while/body/eval_jaxpr/dot_general | solution.py:99
  97.7 2.3 %fusion.67 = f32[2048,256]{1,0:T(8,128)S(1)} fusion(f32[2048,256]{1,0:T(8,128)S(1)} %get-tuple-element.362, s32[512]{0:T(512)S(1)} %bitcast.106, pred[]{:T(512)S(6)} %compare.8, bf16[4,512,256]{2,1,0:T(8,128)(2,1)} %get-tuple-element.370, s32[]{:T(128)S(6)} %copy.74), kind=kOutput, calls=%fused_computation.60.clone.1 | convolution fusion | flops 538968064 | bytes 4458501 | tf_op jit(solution)/shard_map/while/body/eval_jaxpr/dot_general | solution.py:99
  102.0 45.7 %psum.7 = f32[]{:T(128)} all-reduce(f32[]{:T(128)} %convert_reduce_fusion), channel_id=1, replica_groups=mesh['group'=4,'batch'=8] {'group','batch'}, use_global_device_ids=true, to_apply=%region_1.0 | all-reduce | flops 1 | bytes 8 | tf_op jit(solution)/shard_map/psum | solution.py:110
  148.4 1.4 reduce-scatter.2.cloned.1.call-done
  149.8 1.7 %broadcast_multiply_fusion = f32[256,256]{1,0:T(8,128)} fusion(f32[256,256]{1,0:T(8,128)} %reduce-scatter.2.cloned.1.call-done, f32[]{:T(128)S(6)} %div.21), kind=kLoop, calls=%fused_computation.69 | loop fusion | flops 65536 | bytes 524292 | tf_op jit(solution)/shard_map/mul | solution.py:129
  (104 shorter events, 28.6 us)
Async XLA Ops:
  6.5 12.4 %copy-start = (bf16[2048,256]{1,0:T(8,128)(2,1)S(1)}, bf16[2048,256]{1,0:T(8,128)(2,1)}, u32[]{:S(2)}) copy-start(bf16[2048,256]{1,0:T(8,128)(2,1)} %param.14) | copy-start | bytes 3145732
  6.5 12.4 %copy-start.3 = (bf16[256,256]{1,0:T(8,128)(2,1)S(1)}, bf16[256,256]{1,0:T(8,128)(2,1)}, u32[]{:S(2)}) copy-start(bf16[256,256]{1,0:T(8,128)(2,1)} %param.16) | copy-start | bytes 393220
  10.4 49.8 %all-to-all-start = ((s32[4,4,128]{2,1,0:T(4,128)}), s32[4,4,128]{2,1,0:T(4,128)S(1)}, u32[]{:S(2)}, u32[]{:S(2)}) async-start(s32[4,4,128]{2,1,0:T(4,128)} %bitcast.20), calls=%async_computation | async-start | bytes 16384 | tf_op jit(solution)/shard_map/all_to_all | solution.py:120
  18.9 0.9 copy-start.4
  19.8 1.6 copy-start.2
  21.4 1.6 %copy-start.5 = (s32[4]{0:T(128)S(1)}, s32[4]{0:T(128)}, u32[]{:S(2)}) copy-start(s32[4]{0:T(128)} %param.19) | copy-start | bytes 52
  60.2 30.4 %all-to-all-start.1 = ((bf16[16,128,256]{2,1,0:T(8,128)(2,1)}), bf16[16,128,256]{2,1,0:T(8,128)(2,1)}, u32[]{:S(2)}, u32[]{:S(2)}) async-start(bf16[16,128,256]{2,1,0:T(8,128)(2,1)} %gather_fusion.1), calls=%async_computation.1 | async-start | bytes 2097152 | tf_op jit(solution)/shard_map/all_to_all | solution.py:119
  65.3 84.6 %reduce-scatter.2.cloned.1.call-start = ((), (), s32[]{:S(2)}) async-start(), calls=%async_computation.3 | async-start | bytes 2359296 | tf_op jit(solution)/shard_map/reduce_scatter | solution.py:123
  100.0 1.3 copy-start.1
Sparse Core Ops, SparseCore 0:
  101.5 48.2 reduce-scatter.1
where the time goes:
time: 159 us; the launch traced here: 158 us
  blocking collectives  45.7 us (29%)
  local copies, waits for them, and re-layouts  28 us (18%)
  waiting for transfers between devices  26.7 us (17%)
  matrix products  18.7 us (12%)
  between operations  14.1 us (9%)
  starting transfers between devices  11.4 us (7%)
  other arithmetic  7.41 us (5%)
  loops' own time  6.25 us (4%)
    psum x1, blocking collectives, on_device(): lax.psum(jnp.sum(lengths.astype(jnp.float32)), ('group', 'batch'))  45.7 us
    all_to_all x1, waiting for transfers between devices, on_device(): lax.all_to_all(tile_values, 'group', split_axis=0, concat_axis=0, tiled=T...  25.3 us
    dynamic_slice x28, local copies, waits for them, and re-layouts, token_grads(): result = lax.map(one_history, (query, key_rows, value, grad_heads, lengths))  14 us
    dot_general x4, matrix products, add_block(): jnp.dot(onehot, item[0], preferred_element_type=jnp.float32)  9.34 us
    all_to_all x1, starting transfers between devices, on_device(): lax.all_to_all(tile_rows, 'group', split_axis=0, concat_axis=0, tiled=True)  6.35 us
    all_to_all x1, starting transfers between devices, on_device(): lax.all_to_all(tile_values, 'group', split_axis=0, concat_axis=0, tiled=T...  5.09 us
    another operation x4, loops' own time, one_history(): return lax.cond(item[4] <= half_span, short_history, whole_history, item)  3.22 us
  transfers between devices with their start and end apart: 3, of which 2 were waited for; matrix products, arithmetic and copies ran while one was open for 24% of the time, Pallas kernels for 0%

commit v1 on v0

--- a/solution.py
+++ b/solution.py
@@ -8,6 +8,29 @@
 TILE = 128
 SEQ_LEN = 512
 ROWS_DEV = 256
+
+
+def split_up(x, dim, size):
+    dims = x.shape
+    blocks = x.reshape(*dims[:dim], size, dims[dim] // size, *dims[dim + 1 :])
+    return jnp.moveaxis(blocks, dim, 0)
+
+
+def joined_along(blocks, dim):
+    blocks = jnp.moveaxis(blocks, 0, dim)
+    lengths = blocks.shape
+    return blocks.reshape(*lengths[:dim], lengths[dim] * lengths[dim + 1], *lengths[dim + 2 :])
+
+
+def exchange_in_pairs(x, axis, split_dim, concat_dim):
+    size, mine = (lax.axis_size(axis), lax.axis_index(axis))
+    blocks = split_up(x, split_dim, size)
+    done = [blocks[mine]]
+    for turn in range(1, size):
+        sent = blocks[mine ^ turn]
+        done.append(lax.ppermute(sent, axis, [(i, i ^ turn) for i in range(size)]))
+    blocks = jnp.stack(done)[mine ^ jnp.arange(size)]
+    return joined_along(blocks, concat_dim)
 
 
 def sequence_grads(query, key_rows, value, grad_out, count, w_query, w_key, w_value):
@@ -116,7 +139,7 @@
     tile_values = token_grad.reshape(-1, TILE, width)[ranking]
     tile_rows = item_rows.reshape(-1, TILE)[ranking]
     got_values, got_rows = (
-        lax.all_to_all(tile_values, "group", split_axis=0, concat_axis=0, tiled=True),
+        exchange_in_pairs(tile_values, "group", 0, 0),
         lax.all_to_all(tile_rows, "group", split_axis=0, concat_axis=0, tiled=True),
     )
     empty_rows = jnp.zeros((ROWS_DEV * lax.axis_size("batch"), width), jnp.float32)

time: 159 us -> 154 us (0.969)
  waiting for transfers between devices: 26.7 us -> 17 us
  other arithmetic: 7.41 us -> 9.57 us
  local copies, waits for them, and re-layouts: 28 us -> 29.6 us
  blocking collectives: 45.7 us -> 47.3 us
    all_to_all x1 -> x0, waiting for transfers between devices: 25.3 us -> none  [on_device(): lax.all_to_all(tile_values, 'group', split_axis=0, concat_axis=0, tiled=T...]
    all_to_all x1, waiting for transfers between devices: 0.01 us -> 15.9 us  [on_device(): lax.all_to_all(tile_rows, 'group', split_axis=0, concat_axis=0, tiled=True)]
    ppermute x0 -> x3, starting transfers between devices: none -> 5.64 us  [exchange_in_pairs(): done.append(lax.ppermute(sent, axis, [(i, i ^ turn) for i in range(size)]))]
    all_to_all x1 -> x0, starting transfers between devices: 5.09 us -> none  [on_device(): lax.all_to_all(tile_values, 'group', split_axis=0, concat_axis=0, tiled=T...]
    gather x0 -> x1, local copies, waits for them, and re-layouts: none -> 2.81 us  [exchange_in_pairs(): blocks = jnp.stack(done)[mine ^ jnp.arange(size)]]
    another operation x0 -> x1, other arithmetic: none -> 2.28 us  [exchange_in_pairs(): blocks = jnp.stack(done)[mine ^ jnp.arange(size)]]
  transfers between devices with their start and end apart: 3 -> 5, of which waited for: 2 -> 2; matrix products, arithmetic and copies ran while one was open for 24% -> 1% of each run, Pallas kernels for 0% -> 0%
where the time goes in v1:
time: 154 us; the launch traced here: 153 us
  blocking collectives  47.3 us (31%)
  local copies, waits for them, and re-layouts  29.6 us (19%)
  matrix products  18.6 us (12%)
  waiting for transfers between devices  17 us (11%)
  between operations  14.2 us (9%)
  starting transfers between devices  10.7 us (7%)
  other arithmetic  9.57 us (6%)
  loops' own time  6.01 us (4%)
    psum x1, blocking collectives, on_device(): lax.psum(jnp.sum(lengths.astype(jnp.float32)), ('group', 'batch'))  47.3 us
    all_to_all x1, waiting for transfers between devices, on_device(): lax.all_to_all(tile_rows, 'group', split_axis=0, concat_axis=0, tiled=True)  15.9 us
    dynamic_slice x28, local copies, waits for them, and re-layouts, token_grads(): result = lax.map(one_history, (query, key_rows, value, grad_heads, lengths))  13.8 us
    dot_general x4, matrix products, add_block(): jnp.dot(onehot, item[0], preferred_element_type=jnp.float32)  9.34 us
    ppermute x3, starting transfers between devices, exchange_in_pairs(): done.append(lax.ppermute(sent, axis, [(i, i ^ turn) for i in range(size)]))  5.64 us
    all_to_all x1, starting transfers between devices, on_device(): lax.all_to_all(tile_rows, 'group', split_axis=0, concat_axis=0, tiled=True)  5.09 us
    reshape x3, local copies, waits for them, and re-layouts, project(): return jnp.dot(embeds, weight_matrix, preferred_element_type=jnp.float32)...  3.45 us
    another operation x4, loops' own time, one_history(): return lax.cond(item[4] <= half_span, short_history, whole_history, item)  3.1 us
  transfers between devices with their start and end apart: 5, of which 2 were waited for; matrix products, arithmetic and copies ran while one was open for 1% of the time, Pallas kernels for 0%

profile of v1, /device:TPU:0, one launch (start us, length us, event | category | flops | bytes accessed | tf_op | source)
XLA Modules:
  0.0 153.0 jit_solution(9935553093365171313)
XLA Ops:
  6.5 2.0 %sort.17 = (s32[16]{0:T(128)}, s32[16]{0:T(128)S(1)}) sort(s32[16]{0:T(128)} %param.21, s32[16]{0:T(128)S(1)} %iota.52), dimensions={0}, to_apply=%region_6.7 | sort | flops 64 | bytes 256 | tf_op jit(solution)/shard_map/jit(argsort)/sort | solution.py:138
  8.5 1.3 reshape.98
  14.7 33.6 %while.21 = (s32[]{:T(128)}, bf16[4,512,256]{2,1,0:T(8,128)(2,1)}, s32[4]{0:T(128)S(1)}, bf16[4,512,2,128]{3,2,1,0:T(2,128)(2,1)}, bf16[4,512,2,128]{3,2,1,0:T(2...) while((s32[]{:T(128)}, bf16[4,512,256]{2,1,0:T(8,128)(2,1)}, ...), condition=%wide.region_5.6_spmd, body=%wide.region_2.5_spmd.sunk | while | flops 883687936 | bytes 23463240 | solution.py:109
  17.3 1.4 constant_dynamic-slice_fusion.10
  18.8 3.5 %conditional.2 = (bf16[1,512,256]{2,1,0:T(8,128)(2,1)S(1)}) conditional(s32[]{:T(128)} %convert_element_type.105, (bf16[512,2,128]{2,0,1:T(8,128)(2,1)S(1)}, bf16[512,2,128]{2,0,1:T(8,128)(2,1)S(1)}, s32[]{:T(128)}, bf16[512,2,128]{2,0,1:T(8,128)(2,1)S(1)}, bf16[512,2,128]{2,0,1:T(8,128)(2,1)S(1)}, /*index=5*/bf16[256,256]{1,0:T(8,128)(2,1)S(1)}, ...), branch_computations={%region_3.3_spmd, %region_4.4_spmd} | conditional | flops 883687936 | bytes 18744356 | solution.py:107
  25.8 1.4 constant_dynamic-slice_fusion.10
  27.2 3.5 %conditional.2 = (bf16[1,512,256]{2,1,0:T(8,128)(2,1)S(1)}) conditional(s32[]{:T(128)} %convert_element_type.105, (bf16[512,2,128]{2,0,1:T(8,128)(2,1)S(1)}, bf16[512,2,128]{2,0,1:T(8,128)(2,1)S(1)}, s32[]{:T(128)}, bf16[512,2,128]{2,0,1:T(8,128)(2,1)S(1)}, bf16[512,2,128]{2,0,1:T(8,128)(2,1)S(1)}, /*index=5*/bf16[256,256]{1,0:T(8,128)(2,1)S(1)}, ...), branch_computations={%region_3.3_spmd, %region_4.4_spmd} | conditional | flops 883687936 | bytes 18744356 | solution.py:107
  34.2 1.4 constant_dynamic-slice_fusion.10
  35.6 3.5 %conditional.2 = (bf16[1,512,256]{2,1,0:T(8,128)(2,1)S(1)}) conditional(s32[]{:T(128)} %convert_element_type.105, (bf16[512,2,128]{2,0,1:T(8,128)(2,1)S(1)}, bf16[512,2,128]{2,0,1:T(8,128)(2,1)S(1)}, s32[]{:T(128)}, bf16[512,2,128]{2,0,1:T(8,128)(2,1)S(1)}, bf16[512,2,128]{2,0,1:T(8,128)(2,1)S(1)}, /*index=5*/bf16[256,256]{1,0:T(8,128)(2,1)S(1)}, ...), branch_computations={%region_3.3_spmd, %region_4.4_spmd} | conditional | flops 883687936 | bytes 18744356 | solution.py:107
  42.6 1.4 constant_dynamic-slice_fusion.10
  44.1 3.5 %conditional.2 = (bf16[1,512,256]{2,1,0:T(8,128)(2,1)S(1)}) conditional(s32[]{:T(128)} %convert_element_type.105, (bf16[512,2,128]{2,0,1:T(8,128)(2,1)S(1)}, bf16[512,2,128]{2,0,1:T(8,128)(2,1)S(1)}, s32[]{:T(128)}, bf16[512,2,128]{2,0,1:T(8,128)(2,1)S(1)}, bf16[512,2,128]{2,0,1:T(8,128)(2,1)S(1)}, /*index=5*/bf16[256,256]{1,0:T(8,128)(2,1)S(1)}, ...), branch_computations={%region_3.3_spmd, %region_4.4_spmd} | conditional | flops 883687936 | bytes 18744356 | solution.py:107
  48.3 1.9 %gather_fusion.1 = bf16[16,128,256]{2,1,0:T(8,128)(2,1)S(1)} fusion(bf16[16,128,256]{2,1,0:T(8,128)(2,1)} %bitcast.118, s32[1024]{0:T(1024)S(1)} %pad_clamp_fusion.1), kind=kCustom, calls=%fused_computation.1 | custom fusion | bytes 2097216 | tf_op jit(solution)/shard_map/gather | solution.py:139
  51.1 5.1 %collective-permute-start.2 = (bf16[4,128,256]{2,1,0:T(8,128)(2,1)}, bf16[4,128,256]{2,1,0:T(8,128)(2,1)}, u32[]{:S(2)}, u32[]{:S(2)}) collective-permute-start(bf16[4,128,256]{2,1,0:T(8,128)(2,1)} %get-tuple-element.226), channel_id=1, source_target_pairs={{0,24},{8,16},{16,8},{24,0},{1,25},{9,17},{17,9},{25,1},{2,26},{10... | collective-permute-start | bytes 786440 | tf_op jit(solution)/shard_map/ppermute | solution.py:31
  57.9 5.1 %all-to-all-start = ((s32[4,4,128]{2,1,0:T(4,128)}), s32[4,4,128]{2,1,0:T(4,128)S(1)}, u32[]{:S(2)}, u32[]{:S(2)}) async-start(s32[4,4,128]{2,1,0:T(4,128)} %bitcast.20), calls=%async_computation | async-start | bytes 16384 | tf_op jit(solution)/shard_map/all_to_all | solution.py:143
  63.0 15.9 %all-to-all-done = s32[4,4,128]{2,1,0:T(4,128)S(1)} async-done(((s32[4,4,128]{2,1,0:T(4,128)}), s32[4,4,128]{2,1,0:T(4,128)S(1)}, u32[]{:S(2)}, u32[]{:S(2)}) %all-to-all-start) | async-done | bytes 8224 | tf_op jit(solution)/shard_map/all_to_all | solution.py:143
  79.0 2.3 %pad_maximum_fusion = bf16[4,4,128,256]{3,2,1,0:T(8,128)(2,1)} fusion(bf16[1,4,128,256]{3,2,1,0:T(8,128)(2,1)} %bitcast.28, bf16[1,4,128,256]{3,2,1,0:T(8,128)(2,1)} %bitcast.26, bf16[1,4,128,256]{3,2,1,0:T(8,128)(2,1)} %bitcast.24, bf16[1,4,128,256]{3,2,1,0:T(8,128)(2,1)S(1)} %get-tuple-element.225), kind=kLoop, calls=%fused_computation.70 | loop fusion | flops 1572864 | bytes 2097152 | tf_op jit(solution)/shard_map/stack | solution.py:32
  81.2 2.8 %gather_fusion.2 = bf16[4,4,128,256]{3,2,1,0:T(8,128)(2,1)} fusion(bf16[4,4,128,256]{3,2,1,0:T(8,128)(2,1)} %pad_maximum_fusion, s32[1024]{0:T(1024)S(1)} %pad_clamp_fusion), kind=kCustom, calls=%fused_computation.2 | custom fusion | bytes 2097168 | tf_op jit(solution)/shard_map/gather | solution.py:32
  84.0 9.5 %while.22 = (s32[]{:T(128)}, f32[2048,256]{1,0:T(8,128)S(1)}, s32[4,512]{1,0:T(4,128)S(1)}, bf16[4,512,256]{2,1,0:T(8,128)(2,1)}, s32[]{:T(128)}, /*index=5*/s32[]{:T(128)}) while((s32[]{:T(128)}, f32[2048,256]{1,0:T(8,128)S(1)}, s32[4,512]{1,0:T(4,128)S(1)}, bf16[4,512,256]{2,1,0:T(8,128)(2,1)}, s32[]{:T(128)}, ...), condition=%wide.region_8.9_spmd.clone, body=%wide.region_7.8_spmd.clone.sunk | while | flops 538968064 | bytes 4462687 | solution.py:128
  84.0 2.3 %fusion.68 = f32[2048,256]{1,0:T(8,128)S(1)} fusion(f32[2048,256]{1,0:T(8,128)S(1)} %get-tuple-element.366, s32[512]{0:T(512)S(1)} %bitcast.120, pred[]{:T(512)S(6)} %compare.8, bf16[4,512,256]{2,1,0:T(8,128)(2,1)} %get-tuple-element.374, s32[]{:T(128)S(6)} %copy.74), kind=kOutput, calls=%fused_computation.61.clone.1 | convolution fusion | flops 538968064 | bytes 4458501 | tf_op jit(solution)/shard_map/while/body/eval_jaxpr/dot_general | solution.py:122
  86.4 2.3 %fusion.68 = f32[2048,256]{1,0:T(8,128)S(1)} fusion(f32[2048,256]{1,0:T(8,128)S(1)} %get-tuple-element.366, s32[512]{0:T(512)S(1)} %bitcast.120, pred[]{:T(512)S(6)} %compare.8, bf16[4,512,256]{2,1,0:T(8,128)(2,1)} %get-tuple-element.374, s32[]{:T(128)S(6)} %copy.74), kind=kOutput, calls=%fused_computation.61.clone.1 | convolution fusion | flops 538968064 | bytes 4458501 | tf_op jit(solution)/shard_map/while/body/eval_jaxpr/dot_general | solution.py:122
  88.8 2.3 %fusion.68 = f32[2048,256]{1,0:T(8,128)S(1)} fusion(f32[2048,256]{1,0:T(8,128)S(1)} %get-tuple-element.366, s32[512]{0:T(512)S(1)} %bitcast.120, pred[]{:T(512)S(6)} %compare.8, bf16[4,512,256]{2,1,0:T(8,128)(2,1)} %get-tuple-element.374, s32[]{:T(128)S(6)} %copy.74), kind=kOutput, calls=%fused_computation.61.clone.1 | convolution fusion | flops 538968064 | bytes 4458501 | tf_op jit(solution)/shard_map/while/body/eval_jaxpr/dot_general | solution.py:122
  91.2 2.3 %fusion.68 = f32[2048,256]{1,0:T(8,128)S(1)} fusion(f32[2048,256]{1,0:T(8,128)S(1)} %get-tuple-element.366, s32[512]{0:T(512)S(1)} %bitcast.120, pred[]{:T(512)S(6)} %compare.8, bf16[4,512,256]{2,1,0:T(8,128)(2,1)} %get-tuple-element.374, s32[]{:T(128)S(6)} %copy.74), kind=kOutput, calls=%fused_computation.61.clone.1 | convolution fusion | flops 538968064 | bytes 4458501 | tf_op jit(solution)/shard_map/while/body/eval_jaxpr/dot_general | solution.py:122
  95.5 47.3 %psum.7 = f32[]{:T(128)} all-reduce(f32[]{:T(128)} %convert_reduce_fusion), channel_id=1, replica_groups=mesh['group'=4,'batch'=8] {'group','batch'}, use_global_device_ids=true, to_apply=%region_1.0 | all-reduce | flops 1 | bytes 8 | tf_op jit(solution)/shard_map/psum | solution.py:133
  144.5 1.7 %broadcast_multiply_fusion = f32[256,256]{1,0:T(8,128)} fusion(f32[256,256]{1,0:T(8,128)} %reduce-scatter.2.cloned.1.call-done, f32[]{:T(128)S(6)} %div.21), kind=kLoop, calls=%fused_computation.74 | loop fusion | flops 65536 | bytes 524292 | tf_op jit(solution)/shard_map/mul | solution.py:152
  (115 shorter events, 32.6 us)
Async XLA Ops:
  6.5 3.4 %copy-start = (bf16[2048,256]{1,0:T(8,128)(2,1)S(1)}, bf16[2048,256]{1,0:T(8,128)(2,1)}, u32[]{:S(2)}) copy-start(bf16[2048,256]{1,0:T(8,128)(2,1)} %param.14) | copy-start | bytes 3145732
  6.5 3.4 %copy-start.3 = (bf16[256,256]{1,0:T(8,128)(2,1)S(1)}, bf16[256,256]{1,0:T(8,128)(2,1)}, u32[]{:S(2)}) copy-start(bf16[256,256]{1,0:T(8,128)(2,1)} %param.16) | copy-start | bytes 393220
  9.9 1.6 %copy-start.4 = (bf16[256,256]{1,0:T(8,128)(2,1)S(1)}, bf16[256,256]{1,0:T(8,128)(2,1)}, u32[]{:S(2)}) copy-start(bf16[256,256]{1,0:T(8,128)(2,1)} %param.17) | copy-start | bytes 393220
  11.5 1.6 %copy-start.2 = (bf16[256,256]{1,0:T(8,128)(2,1)S(1)}, bf16[256,256]{1,0:T(8,128)(2,1)}, u32[]{:S(2)}) copy-start(bf16[256,256]{1,0:T(8,128)(2,1)} %param.18) | copy-start | bytes 393220
  13.1 1.6 %copy-start.6 = (s32[4]{0:T(128)S(1)}, s32[4]{0:T(128)}, u32[]{:S(2)}) copy-start(s32[4]{0:T(128)} %param.19) | copy-start | bytes 52
  48.3 8.4 %copy-start.5 = (s32[2048]{0:T(1024)S(1)}, s32[2048]{0:T(1024)}, u32[]{:S(2)}) copy-start(s32[2048]{0:T(1024)} %param.20) | copy-start | bytes 24580
  51.1 27.9 %collective-permute-start.2 = (bf16[4,128,256]{2,1,0:T(8,128)(2,1)}, bf16[4,128,256]{2,1,0:T(8,128)(2,1)}, u32[]{:S(2)}, u32[]{:S(2)}) collective-permute-start(bf16[4,128,256]{2,1,0:T(8,128)(2,1)} %get-tuple-element.226), channel_id=1, source_target_pairs={{0,24},{8,16},{16,8},{24,0},{1,25},{9,17},{17,9},{25,1},{2,26},{10... | collective-permute-start | bytes 786440 | tf_op jit(solution)/shard_map/ppermute | solution.py:31
  56.2 22.8 %collective-permute-start.1 = (bf16[4,128,256]{2,1,0:T(8,128)(2,1)}, bf16[4,128,256]{2,1,0:T(8,128)(2,1)}, u32[]{:S(2)}, u32[]{:S(2)}) collective-permute-start(bf16[4,128,256]{2,1,0:T(8,128)(2,1)} %get-tuple-element.227), channel_id=1, source_target_pairs={{0,16},{8,24},{16,0},{24,8},{1,17},{9,25},{17,1},{25,9},{2,18},{10... | collective-permute-start | bytes 786440 | tf_op jit(solution)/shard_map/ppermute | solution.py:31
  56.2 22.8 %collective-permute-start = (bf16[4,128,256]{2,1,0:T(8,128)(2,1)}, bf16[4,128,256]{2,1,0:T(8,128)(2,1)}, u32[]{:S(2)}, u32[]{:S(2)}) collective-permute-start(bf16[4,128,256]{2,1,0:T(8,128)(2,1)} %get-tuple-element.228), channel_id=1, source_target_pairs={{0,8},{8,0},{16,24},{24,16},{1,9},{9,1},{17,25},{25,17},{2,10},{10... | collective-permute-start | bytes 786440 | tf_op jit(solution)/shard_map/ppermute | solution.py:31
  57.9 21.1 %all-to-all-start = ((s32[4,4,128]{2,1,0:T(4,128)}), s32[4,4,128]{2,1,0:T(4,128)S(1)}, u32[]{:S(2)}, u32[]{:S(2)}) async-start(s32[4,4,128]{2,1,0:T(4,128)} %bitcast.20), calls=%async_computation | async-start | bytes 16384 | tf_op jit(solution)/shard_map/all_to_all | solution.py:143
  63.0 81.5 %reduce-scatter.2.cloned.1.call-start = ((), (), s32[]{:S(2)}) async-start(), calls=%async_computation.2 | async-start | bytes 2359296 | tf_op jit(solution)/shard_map/reduce_scatter | solution.py:146
  93.5 1.4 copy-start.1
Sparse Core Ops, SparseCore 0:
  95.0 49.3 reduce-scatter.1
